TPU v7x, 32 devices: a whole 2x2x4 slice. The times are simulated.
32 devices in a mesh: row: 4 (over y, x), rhs: 8 (over z, core).
Axes of the slice: x: 2, y: 2, z: 4, core: 2. Of those that a mesh axis runs over, the one named last changes fastest.
Arguments:
- factor: float32 [3072, 12, 256], P('row', None, 'rhs'), as said below
- inverses: float32 [12, 256, 256], P('row'), as said below
- right_side: float32 [3072, 4096], P('row', 'rhs'), may hold values from -6 to 6
Outputs:
- solution: float32 [3072, 4096], P('row', 'rhs')
Inputs may be any that keep to these rules, and one draw needn't show every extreme that they name: factor[i, j, c] is zero unless j is less than i // 256. Each inverses[p] is lower triangular with a positive diagonal.
All inputs are finite; a program needn't handle non-finite values.
Results may differ from a plain program's by a relative error of at most 0.0001.
Values sent between devices are 32-bit elements; how exact they have to be, the bound alone decides.
No kernel may reach another device: no remote copies, remote signals or barrier semaphores. Data moves between devices by JAX's collectives and lax.ppermute only.
A program may use at most 128 MiB of HBM per device.

v0:
```python
import jax
import jax.numpy as jnp
from jax import lax
from jax.sharding import PartitionSpec as P


def from_root(block, axis, owner):
    block = jnp.where(lax.axis_index(axis) == owner, block, jnp.zeros_like(block))
    return lax.psum(block, axis)


def mult(left, right):
    return jnp.dot(left, right, preferred_element_type=jnp.float32, precision=lax.Precision.HIGHEST)


def body(factor, inverses, right_side):
    block = right_side.shape[0]
    panel = inverses.shape[1]
    per_block = inverses.shape[0]
    rounds = lax.axis_size("row")
    mine = lax.axis_index("row")
    gathered = lax.all_gather(factor, "rhs", axis=2, tiled=True)

    def fetch(first, count):
        return lax.dynamic_slice_in_dim(gathered, first, count, 1)

    def apply_tiles(residual, tiles, solved):
        return residual - mult(tiles.reshape(block, -1), solved)

    solution = jnp.zeros_like(right_side)

    def step_block(index, state):
        residual, solution = state
        tiles = fetch(index * per_block, per_block)
        working = residual
        pieces = []
        for inner in range(per_block):
            solved_part = mult(inverses[inner], working[inner * panel : (inner + 1) * panel])
            pieces.append(solved_part)
            working = working - mult(tiles[:, inner, :], solved_part)
        solved = from_root(jnp.concatenate(pieces, axis=0), "row", index)
        residual = apply_tiles(residual, tiles, solved)
        solution = jnp.where(mine == index, solved, solution)
        return (residual, solution)

    residual, solution = lax.fori_loop(0, rounds, step_block, (right_side, solution))
    return solution


def solution(mesh):
    placed = (P("row", None, "rhs"), P("row", None, None), P("row", "rhs"))
    return jax.shard_map(
        body, mesh=mesh, in_specs=placed, out_specs=P("row", "rhs"), check_vma=False
    )
```

profile of v0, /device:TPU:0, one launch (start us, length us, event | category | flops | bytes accessed | tf_op | source)
XLA Modules:
  0.0 417.8 jit_solution(4897587918877244173)
XLA Ops:
  6.5 0.7 all-gather.2.cloned.1.call-update
  7.3 95.1 %all-gather.2.cloned.1.call-done = f32[768,12,256]{0,2,1:T(8,128)} async-done(((f32[768,12,32]{0,2,1:T(8,128)}), f32[768,12,256]{0,2,1:T(8,128)}) %all-gather.2.cloned.1.call-update) | async-done | bytes 9437200 | tf_op jit(solution)/shard_map/all_gather | solution.py:22
  102.4 307.8 %while.16 = (s32[]{:T(128)}, f32[768,512]{1,0:T(8,128)S(1)}, f32[768,512]{1,0:T(8,128)S(1)}, f32[768,12,256]{0,2,1:T(8,128)}, f32[3,256,256]{2,1,0:T(8,128)}, /*...) while((s32[]{:T(128)}, f32[768,512]{1,0:T(8,128)S(1)}, ...), condition=%wide.region_2.3_spmd.clone, body=%wide.region_0.2_spmd.clone.sunk | while | flops 7251034112 | bytes 50332000 | solution.py:46
  102.4 1.6 fusion.39
  104.0 2.7 convolution_subtract_fusion.4
  107.3 2.6 fusion.41
  110.6 1.3 maximum_select_fusion.2
  111.9 3.2 constant_dynamic-slice_fusion.2
  115.1 56.1 %all-reduce.2.cloned.1.call-done = f32[768,512]{1,0:T(8,128)} async-done(((f32[768,512]{1,0:T(8,128)}), f32[768,512]{1,0:T(8,128)}) %all-reduce.2.cloned.1.call-update) | async-done | bytes 1572880 | tf_op jit(solution)/shard_map/while/body/eval_jaxpr/psum | solution.py:9
  171.2 6.4 %convolution_subtract_fusion.5 = f32[768,512]{1,0:T(8,128)S(1)} fusion(f32[768,512]{1,0:T(8,128)S(1)} %get-tuple-element.198, f32[768,768]{0,1:T(8,128)} %bitcast.47, f32[768,512]{1,0:T(8,128)} %all-reduce.2.cloned.1.call-done), kind=kOutput, calls=%fused_computation.3.clone.1 | convolution fusion | flops 3624271872 | bytes 7077888 | tf_op jit(solution)/shard_map/while/body/eval_jaxpr/dot_general | solution.py:13
  178.2 1.6 fusion.39
  179.8 2.7 convolution_subtract_fusion.4
  183.1 2.6 fusion.41
  186.3 1.3 maximum_select_fusion.2
  187.7 3.2 constant_dynamic-slice_fusion.2
  190.9 57.7 %all-reduce.2.cloned.1.call-done = f32[768,512]{1,0:T(8,128)} async-done(((f32[768,512]{1,0:T(8,128)}), f32[768,512]{1,0:T(8,128)}) %all-reduce.2.cloned.1.call-update) | async-done | bytes 1572880 | tf_op jit(solution)/shard_map/while/body/eval_jaxpr/psum | solution.py:9
  248.5 6.4 %convolution_subtract_fusion.5 = f32[768,512]{1,0:T(8,128)S(1)} fusion(f32[768,512]{1,0:T(8,128)S(1)} %get-tuple-element.198, f32[768,768]{0,1:T(8,128)} %bitcast.47, f32[768,512]{1,0:T(8,128)} %all-reduce.2.cloned.1.call-done), kind=kOutput, calls=%fused_computation.3.clone.1 | convolution fusion | flops 3624271872 | bytes 7077888 | tf_op jit(solution)/shard_map/while/body/eval_jaxpr/dot_general | solution.py:13
  255.5 1.6 fusion.39
  257.1 2.7 convolution_subtract_fusion.4
  260.4 2.6 fusion.41
  263.7 1.3 maximum_select_fusion.2
  265.0 3.2 constant_dynamic-slice_fusion.2
  268.2 57.7 %all-reduce.2.cloned.1.call-done = f32[768,512]{1,0:T(8,128)} async-done(((f32[768,512]{1,0:T(8,128)}), f32[768,512]{1,0:T(8,128)}) %all-reduce.2.cloned.1.call-update) | async-done | bytes 1572880 | tf_op jit(solution)/shard_map/while/body/eval_jaxpr/psum | solution.py:9
  325.9 6.4 %convolution_subtract_fusion.5 = f32[768,512]{1,0:T(8,128)S(1)} fusion(f32[768,512]{1,0:T(8,128)S(1)} %get-tuple-element.198, f32[768,768]{0,1:T(8,128)} %bitcast.47, f32[768,512]{1,0:T(8,128)} %all-reduce.2.cloned.1.call-done), kind=kOutput, calls=%fused_computation.3.clone.1 | convolution fusion | flops 3624271872 | bytes 7077888 | tf_op jit(solution)/shard_map/while/body/eval_jaxpr/dot_general | solution.py:13
  332.9 1.6 fusion.39
  334.5 2.7 convolution_subtract_fusion.4
  337.8 2.6 fusion.41
  341.0 1.3 maximum_select_fusion.2
  342.4 3.2 constant_dynamic-slice_fusion.2
  345.6 57.7 %all-reduce.2.cloned.1.call-done = f32[768,512]{1,0:T(8,128)} async-done(((f32[768,512]{1,0:T(8,128)}), f32[768,512]{1,0:T(8,128)}) %all-reduce.2.cloned.1.call-update) | async-done | bytes 1572880 | tf_op jit(solution)/shard_map/while/body/eval_jaxpr/psum | solution.py:9
  403.3 6.4 %convolution_subtract_fusion.5 = f32[768,512]{1,0:T(8,128)S(1)} fusion(f32[768,512]{1,0:T(8,128)S(1)} %get-tuple-element.198, f32[768,768]{0,1:T(8,128)} %bitcast.47, f32[768,512]{1,0:T(8,128)} %all-reduce.2.cloned.1.call-done), kind=kOutput, calls=%fused_computation.3.clone.1 | convolution fusion | flops 3624271872 | bytes 7077888 | tf_op jit(solution)/shard_map/while/body/eval_jaxpr/dot_general | solution.py:13
  410.2 1.1 copy-done.2
  (41 shorter events, 7.3 us)
Async XLA Ops:
  6.5 95.9 %copy-start = (f32[768,512]{1,0:T(8,128)S(1)}, f32[768,512]{1,0:T(8,128)}, u32[]{:S(2)}) copy-start(f32[768,512]{1,0:T(8,128)} %param.7) | copy-start | bytes 4718596
  6.5 95.9 %all-gather.2.cloned.1.call-start = ((), (), s32[]{:S(2)}) async-start(), calls=%async_computation | async-start | bytes 10616832 | tf_op jit(solution)/shard_map/all_gather | solution.py:22
  102.4 68.8 %all-reduce.2.cloned.1.call-start = ((), (), s32[]{:S(2)}) async-start(), calls=%async_computation.1 | async-start | bytes 3145728 | tf_op jit(solution)/shard_map/while/body/eval_jaxpr/psum | solution.py:9
  104.0 2.7 copy-start.3
  171.2 6.4 %copy-start.1 = (f32[768,512]{1,0:T(8,128)S(1)}, f32[768,512]{1,0:T(8,128)}, u32[]{:S(2)}) copy-start(f32[768,512]{1,0:T(8,128)} %all-reduce.2.cloned.1.call-done) | copy-start | bytes 4718596 | tf_op jit(solution)/shard_map/while
  178.1 70.4 %all-reduce.2.cloned.1.call-start = ((), (), s32[]{:S(2)}) async-start(), calls=%async_computation.1 | async-start | bytes 3145728 | tf_op jit(solution)/shard_map/while/body/eval_jaxpr/psum | solution.py:9
  179.7 2.7 copy-start.3
  248.5 6.4 %copy-start.1 = (f32[768,512]{1,0:T(8,128)S(1)}, f32[768,512]{1,0:T(8,128)}, u32[]{:S(2)}) copy-start(f32[768,512]{1,0:T(8,128)} %all-reduce.2.cloned.1.call-done) | copy-start | bytes 4718596 | tf_op jit(solution)/shard_map/while
  255.5 70.4 %all-reduce.2.cloned.1.call-start = ((), (), s32[]{:S(2)}) async-start(), calls=%async_computation.1 | async-start | bytes 3145728 | tf_op jit(solution)/shard_map/while/body/eval_jaxpr/psum | solution.py:9
  257.1 2.7 copy-start.3
  325.9 6.4 %copy-start.1 = (f32[768,512]{1,0:T(8,128)S(1)}, f32[768,512]{1,0:T(8,128)}, u32[]{:S(2)}) copy-start(f32[768,512]{1,0:T(8,128)} %all-reduce.2.cloned.1.call-done) | copy-start | bytes 4718596 | tf_op jit(solution)/shard_map/while
  332.8 70.4 %all-reduce.2.cloned.1.call-start = ((), (), s32[]{:S(2)}) async-start(), calls=%async_computation.1 | async-start | bytes 3145728 | tf_op jit(solution)/shard_map/while/body/eval_jaxpr/psum | solution.py:9
  334.5 2.7 copy-start.3
  403.3 6.4 %copy-start.1 = (f32[768,512]{1,0:T(8,128)S(1)}, f32[768,512]{1,0:T(8,128)}, u32[]{:S(2)}) copy-start(f32[768,512]{1,0:T(8,128)} %all-reduce.2.cloned.1.call-done) | copy-start | bytes 4718596 | tf_op jit(solution)/shard_map/while
  410.2 1.1 copy-start.2
Sparse Core Ops, SparseCore 0:
  8.9 93.4 all-gather.1
  112.0 59.1 all-reduce.1
  187.8 60.7 all-reduce.1
  265.1 60.7 all-reduce.1
  342.5 60.7 all-reduce.1
where the time goes:
time: 418 us
  waiting for transfers between devices  325 us (78%)
  matrix products  58 us (14%)
  local copies, waits for them, and re-layouts  14 us (3%)
  between operations  13.1 us (3%)
  other arithmetic  7.15 us (2%)
    psum x4, waiting for transfers between devices, from_root(): return lax.psum(block, axis)  229 us
    all_gather x1, waiting for transfers between devices, body(): gathered = lax.all_gather(factor, 'rhs', axis=2, tiled=True)  95.1 us
    dot_general x24, matrix products, mult(): jnp.dot(left, right, preferred_element_type=jnp.float32, precision=lax.Pr...  58 us
    dynamic_slice x4, local copies, waits for them, and re-layouts, fetch(): return lax.dynamic_slice_in_dim(gathered, first, count, 1)  12.8 us
  transfers between devices with their start and end apart: 5, of which 5 were waited for; matrix products, arithmetic and copies ran while one was open for 3% of the time, Pallas kernels for 0%

commit v1 on v0

--- a/solution.py
+++ b/solution.py
@@ -19,7 +19,7 @@
     per_block = inverses.shape[0]
     rounds = lax.axis_size("row")
     mine = lax.axis_index("row")
-    gathered = lax.all_gather(factor, "rhs", axis=2, tiled=True)
+    gathered = jnp.concatenate(lax.all_gather(factor, "rhs"), axis=2)
 
     def fetch(first, count):
         return lax.dynamic_slice_in_dim(gathered, first, count, 1)

time: 418 us -> 449 us (1.074)
  local copies, waits for them, and re-layouts: 14 us -> 36.4 us
  matrix products: 58 us -> 65.9 us
    while x16 -> x32, local copies, waits for them, and re-layouts: 0.04 us -> 9.16 us
    dot_general x24, matrix products: 58 us -> 65.9 us  [mult(): jnp.dot(left, right, preferred_element_type=jnp.float32, precision=lax.Pr...]
    unnamed x4 -> x3, local copies, waits for them, and re-layouts: 1.14 us -> 7.9 us
    reshape x0 -> x1, local copies, waits for them, and re-layouts: none -> 6.47 us  [body(): gathered = jnp.concatenate(lax.all_gather(factor, 'rhs'), axis=2)]
where the time goes in v1:
time: 449 us; the launch traced here: 448 us
  waiting for transfers between devices  325 us (72%)
  matrix products  65.9 us (15%)
  local copies, waits for them, and re-layouts  36.4 us (8%)
  between operations  13.1 us (3%)
  other arithmetic  7.15 us (2%)
    psum x4, waiting for transfers between devices, from_root(): return lax.psum(block, axis)  229 us
    all_gather x1, waiting for transfers between devices, body(): gathered = jnp.concatenate(lax.all_gather(factor, 'rhs'), axis=2)  95.1 us
    dot_general x24, matrix products, mult(): jnp.dot(left, right, preferred_element_type=jnp.float32, precision=lax.Pr...  65.9 us
    dynamic_slice x4, local copies, waits for them, and re-layouts, fetch(): return lax.dynamic_slice_in_dim(gathered, first, count, 1)  12.9 us
    while x32, local copies, waits for them, and re-layouts  9.16 us
  transfers between devices with their start and end apart: 5, of which 5 were waited for; matrix products, arithmetic and copies ran while one was open for 3% of the time, Pallas kernels for 0%

profile of v1, /device:TPU:0, one launch (start us, length us, event | category | flops | bytes accessed | tf_op | source)
XLA Modules:
  0.0 448.0 jit_solution(14737215861681981530)
XLA Ops:
  7.3 95.1 %all-gather.3.cloned.1.call-done = f32[6144,12,32]{0,2,1:T(8,128)} async-done(((f32[768,12,32]{0,2,1:T(8,128)}), f32[6144,12,32]{0,2,1:T(8,128)}) %all-gather.3.cloned.1.call-update) | async-done | bytes 9437200 | tf_op jit(solution)/shard_map/all_gather | solution.py:22
  102.4 7.9 %copy.6 = f32[48,8,8,768]{3,2,1,0:T(8,128)S(1)} copy(f32[48,8,8,768]{3,1,2,0:T(8,128)} %bitcast.60) | data formatting | bytes 18874368
  110.3 6.5 %copy.5 = f32[768,12,8,32]{0,3,2,1:T(8,128)} copy(f32[768,12,8,32]{0,2,3,1:T(8,128)S(1)} %bitcast.59) | data formatting | bytes 18874368 | tf_op jit(solution)/shard_map/reshape | solution.py:22
  116.8 324.7 %while.16 = (s32[]{:T(128)}, f32[768,512]{1,0:T(8,128)S(1)}, f32[768,512]{1,0:T(8,128)}, f32[768,12,256]{0,2,1:T(8,128)}, f32[3,256,256]{2,1,0:T(8,128)}, /*inde...) while((s32[]{:T(128)}, f32[768,512]{1,0:T(8,128)S(1)}, ...), condition=%wide.region_2.3_spmd.clone, body=%wide.region_0.2_spmd.clone.sunk | while | flops 7251034112 | bytes 66060684 | solution.py:46
  118.3 2.6 convolution_subtract_fusion.4
  122.1 1.6 fusion.40
  123.7 2.6 fusion.41
  126.3 1.8 convolution_bitcast_fusion.2
  129.4 3.2 constant_dynamic-slice_fusion.2
  132.6 56.1 %all-reduce.2.cloned.1.call-done = f32[768,512]{1,0:T(8,128)} async-done(((f32[768,512]{1,0:T(8,128)}), f32[768,512]{1,0:T(8,128)}) %all-reduce.2.cloned.1.call-update) | async-done | bytes 1572880 | tf_op jit(solution)/shard_map/while/body/eval_jaxpr/psum | solution.py:9
  188.7 6.4 %convolution_subtract_fusion.5 = f32[768,512]{1,0:T(8,128)S(1)} fusion(f32[768,512]{1,0:T(8,128)S(1)} %get-tuple-element.198, f32[768,768]{0,1:T(8,128)} %bitcast.56, f32[768,512]{1,0:T(8,128)} %all-reduce.2.cloned.1.call-done), kind=kOutput, calls=%fused_computation.3.clone.1 | convolution fusion | flops 3624271872 | bytes 7077888 | tf_op jit(solution)/shard_map/while/body/eval_jaxpr/dot_general | solution.py:13
  198.3 2.6 convolution_subtract_fusion.4
  202.1 1.6 fusion.40
  203.7 2.6 fusion.41
  206.3 1.8 convolution_bitcast_fusion.2
  209.4 3.2 constant_dynamic-slice_fusion.2
  212.6 57.6 %all-reduce.2.cloned.1.call-done = f32[768,512]{1,0:T(8,128)} async-done(((f32[768,512]{1,0:T(8,128)}), f32[768,512]{1,0:T(8,128)}) %all-reduce.2.cloned.1.call-update) | async-done | bytes 1572880 | tf_op jit(solution)/shard_map/while/body/eval_jaxpr/psum | solution.py:9
  270.3 6.4 %convolution_subtract_fusion.5 = f32[768,512]{1,0:T(8,128)S(1)} fusion(f32[768,512]{1,0:T(8,128)S(1)} %get-tuple-element.198, f32[768,768]{0,1:T(8,128)} %bitcast.56, f32[768,512]{1,0:T(8,128)} %all-reduce.2.cloned.1.call-done), kind=kOutput, calls=%fused_computation.3.clone.1 | convolution fusion | flops 3624271872 | bytes 7077888 | tf_op jit(solution)/shard_map/while/body/eval_jaxpr/dot_general | solution.py:13
  279.9 2.6 convolution_subtract_fusion.4
  283.7 1.6 fusion.40
  285.3 2.6 fusion.41
  287.8 1.8 convolution_bitcast_fusion.2
  291.0 3.2 constant_dynamic-slice_fusion.2
  294.2 57.6 %all-reduce.2.cloned.1.call-done = f32[768,512]{1,0:T(8,128)} async-done(((f32[768,512]{1,0:T(8,128)}), f32[768,512]{1,0:T(8,128)}) %all-reduce.2.cloned.1.call-update) | async-done | bytes 1572880 | tf_op jit(solution)/shard_map/while/body/eval_jaxpr/psum | solution.py:9
  351.8 6.4 %convolution_subtract_fusion.5 = f32[768,512]{1,0:T(8,128)S(1)} fusion(f32[768,512]{1,0:T(8,128)S(1)} %get-tuple-element.198, f32[768,768]{0,1:T(8,128)} %bitcast.56, f32[768,512]{1,0:T(8,128)} %all-reduce.2.cloned.1.call-done), kind=kOutput, calls=%fused_computation.3.clone.1 | convolution fusion | flops 3624271872 | bytes 7077888 | tf_op jit(solution)/shard_map/while/body/eval_jaxpr/dot_general | solution.py:13
  361.5 2.6 convolution_subtract_fusion.4
  365.2 1.6 fusion.40
  366.8 2.6 fusion.41
  369.4 1.8 convolution_bitcast_fusion.2
  372.5 3.2 constant_dynamic-slice_fusion.2
  375.8 57.6 %all-reduce.2.cloned.1.call-done = f32[768,512]{1,0:T(8,128)} async-done(((f32[768,512]{1,0:T(8,128)}), f32[768,512]{1,0:T(8,128)}) %all-reduce.2.cloned.1.call-update) | async-done | bytes 1572880 | tf_op jit(solution)/shard_map/while/body/eval_jaxpr/psum | solution.py:9
  433.4 6.4 %convolution_subtract_fusion.5 = f32[768,512]{1,0:T(8,128)S(1)} fusion(f32[768,512]{1,0:T(8,128)S(1)} %get-tuple-element.198, f32[768,768]{0,1:T(8,128)} %bitcast.56, f32[768,512]{1,0:T(8,128)} %all-reduce.2.cloned.1.call-done), kind=kOutput, calls=%fused_computation.3.clone.1 | convolution fusion | flops 3624271872 | bytes 7077888 | tf_op jit(solution)/shard_map/while/body/eval_jaxpr/dot_general | solution.py:13
  (57 shorter events, 23.3 us)
Async XLA Ops:
  6.5 95.9 %all-gather.3.cloned.1.call-start = ((), (), s32[]{:S(2)}) async-start(), calls=%async_computation | async-start | bytes 10616832 | tf_op jit(solution)/shard_map/all_gather | solution.py:22
  110.3 6.5 %copy-start = (f32[768,512]{1,0:T(8,128)S(1)}, f32[768,512]{1,0:T(8,128)}, u32[]{:S(2)}) copy-start(f32[768,512]{1,0:T(8,128)} %param.7) | copy-start | bytes 4718596
  116.8 71.9 %all-reduce.2.cloned.1.call-start = ((), (), s32[]{:S(2)}) async-start(), calls=%async_computation.1 | async-start | bytes 3145728 | tf_op jit(solution)/shard_map/while/body/eval_jaxpr/psum | solution.py:9
  120.9 1.2 copy-start.2
  188.7 6.4 %copy-start.1 = (f32[768,512]{1,0:T(8,128)S(1)}, f32[768,512]{1,0:T(8,128)}, u32[]{:S(2)}) copy-start(f32[768,512]{1,0:T(8,128)} %all-reduce.2.cloned.1.call-done) | copy-start | bytes 4718596 | tf_op jit(solution)/shard_map/while
  188.7 6.5 %copy-start.3 = (f32[768,512]{1,0:T(8,128)S(1)}, f32[768,512]{1,0:T(8,128)}, u32[]{:S(2)}) copy-start(f32[768,512]{1,0:T(8,128)} %get-tuple-element.199) | copy-start | bytes 4718596 | tf_op jit(solution)/shard_map/while
  195.6 1.1 copy-start.4
  196.8 73.5 %all-reduce.2.cloned.1.call-start = ((), (), s32[]{:S(2)}) async-start(), calls=%async_computation.1 | async-start | bytes 3145728 | tf_op jit(solution)/shard_map/while/body/eval_jaxpr/psum | solution.py:9
  200.9 1.2 copy-start.2
  270.3 6.4 %copy-start.1 = (f32[768,512]{1,0:T(8,128)S(1)}, f32[768,512]{1,0:T(8,128)}, u32[]{:S(2)}) copy-start(f32[768,512]{1,0:T(8,128)} %all-reduce.2.cloned.1.call-done) | copy-start | bytes 4718596 | tf_op jit(solution)/shard_map/while
  270.3 6.4 %copy-start.3 = (f32[768,512]{1,0:T(8,128)S(1)}, f32[768,512]{1,0:T(8,128)}, u32[]{:S(2)}) copy-start(f32[768,512]{1,0:T(8,128)} %get-tuple-element.199) | copy-start | bytes 4718596 | tf_op jit(solution)/shard_map/while
  277.2 1.1 copy-start.4
  278.4 73.5 %all-reduce.2.cloned.1.call-start = ((), (), s32[]{:S(2)}) async-start(), calls=%async_computation.1 | async-start | bytes 3145728 | tf_op jit(solution)/shard_map/while/body/eval_jaxpr/psum | solution.py:9
  282.5 1.2 copy-start.2
  351.8 6.4 %copy-start.1 = (f32[768,512]{1,0:T(8,128)S(1)}, f32[768,512]{1,0:T(8,128)}, u32[]{:S(2)}) copy-start(f32[768,512]{1,0:T(8,128)} %all-reduce.2.cloned.1.call-done) | copy-start | bytes 4718596 | tf_op jit(solution)/shard_map/while
  351.8 6.4 %copy-start.3 = (f32[768,512]{1,0:T(8,128)S(1)}, f32[768,512]{1,0:T(8,128)}, u32[]{:S(2)}) copy-start(f32[768,512]{1,0:T(8,128)} %get-tuple-element.199) | copy-start | bytes 4718596 | tf_op jit(solution)/shard_map/while
  358.8 1.1 copy-start.4
  359.9 73.5 %all-reduce.2.cloned.1.call-start = ((), (), s32[]{:S(2)}) async-start(), calls=%async_computation.1 | async-start | bytes 3145728 | tf_op jit(solution)/shard_map/while/body/eval_jaxpr/psum | solution.py:9
  364.1 1.2 copy-start.2
  433.4 6.4 %copy-start.1 = (f32[768,512]{1,0:T(8,128)S(1)}, f32[768,512]{1,0:T(8,128)}, u32[]{:S(2)}) copy-start(f32[768,512]{1,0:T(8,128)} %all-reduce.2.cloned.1.call-done) | copy-start | bytes 4718596 | tf_op jit(solution)/shard_map/while
  433.4 6.4 %copy-start.3 = (f32[768,512]{1,0:T(8,128)S(1)}, f32[768,512]{1,0:T(8,128)}, u32[]{:S(2)}) copy-start(f32[768,512]{1,0:T(8,128)} %get-tuple-element.199) | copy-start | bytes 4718596 | tf_op jit(solution)/shard_map/while
  440.4 1.1 copy-start.4
Sparse Core Ops, SparseCore 0:
  8.9 93.4 all-gather.2
  129.5 59.1 all-reduce.1
  209.5 60.7 all-reduce.1
  291.1 60.7 all-reduce.1
  372.6 60.7 all-reduce.1
